TPU v7x, 512 devices: a whole 4x8x8 slice. The times are simulated.
512 devices in a mesh: sub: 128 (over z, y, core), leaf: 4 (over x).
Axes of the slice: x: 4, y: 8, z: 8, core: 2. Of those that a mesh axis runs over, the one named last changes fastest.
Arguments:
- child_row: int32 [256], P('sub'), may hold values from 0 to 255, each once
- counts: int32 [256], P('sub'), may hold values from 1 to 16, as said below
- live_mask: int32 [256, 16, 1326], P('sub', 'leaf'), may hold values 0 or 1
- hand_rank: int32 [256, 16, 1326], P('sub', 'leaf'), may hold values from 0 to 7461
- bet_size: float32 [256, 8], P('sub'), may hold values from 0.25 to 4
- pot_size: float32 [256], P('sub'), may hold values from 4 to 16
- trunk_ranges: float32 [256, 2, 1326], P('sub'), may hold values from 0.05 to 1
- trunk_values: float32 [256, 1326], P('sub'), may hold values from -8 to 8
Outputs:
- root_values: float32 [256, 2, 1326], P('sub')
Inputs may be any that keep to these rules, and one draw needn't show every extreme that they name: Subgame s reads and returns row child_row[s] of the trunk's arrays; every row is named by exactly one subgame. Leaf blocks b < counts[s] of subgame s are used; some subgame uses all 16.
All inputs are finite; a program needn't handle non-finite values. No bound on the sum of `live_mask` on one device may be relied on, other than what follows from the above.
Results may differ from a plain program's by a relative error of at most 0.0004.
Values sent between devices are 32-bit elements; how exact they have to be, the bound alone decides.
No kernel may reach another device: no remote copies, remote signals or barrier semaphores. Data moves between devices by JAX's collectives and lax.ppermute only.
A program may use at most 64 MiB of HBM per device.

v0:
```python
import math

import jax
import jax.numpy as jnp
from jax import lax
from jax.sharding import Mesh
from jax.sharding import PartitionSpec as P

ACT = 8
ITERS = 4
SUB = ("sub_0", "sub_1", "sub_2")


smooth = 0.1


def in_one_piece(arrays, axis, dim, along):
    widths = [math.prod(a.shape[along:]) for a in arrays]
    both = jnp.concatenate(
        [a.reshape(*a.shape[:along], w) for a, w in zip(arrays, widths)], axis=along
    )
    whole = lax.all_gather(both, axis, axis=dim, tiled=True)
    parts = jnp.split(whole, [sum(widths[:k]) for k in range(1, len(widths))], axis=along)
    return tuple((b.reshape(*whole.shape[:along], *a.shape[along:]) for a, b in zip(arrays, parts)))


def sent_to_all(shard, axis):
    copies = jnp.broadcast_to(shard, (lax.axis_size(axis), *shard.shape))
    return lax.all_to_all(copies, axis, split_axis=0, concat_axis=0, tiled=True)


def taken_together(shard, axis):
    everything = sent_to_all(shard, axis)
    return jnp.sum(everything, axis=0)


def split_up(shard, dim, count):
    shape = shard.shape
    parts = shard.reshape(*shape[:dim], count, shape[dim] // count, *shape[dim + 1 :])
    return jnp.moveaxis(parts, dim, 0)


def summed_on_arrival(shard, axis, dim):
    parts = split_up(shard, dim, lax.axis_size(axis))
    arrived = lax.all_to_all(parts, axis, split_axis=0, concat_axis=0, tiled=True)
    return arrived.sum(axis=0)


def summed_rows(shard, axes, dim):
    far, near = axes
    own = summed_on_arrival(split_up(shard, dim, lax.axis_size(far)), near, dim + 1)
    return jnp.sum(lax.all_to_all(own, far, 0, 0, tiled=True), axis=0)


def in_order(parts, dim):
    parts = jnp.moveaxis(parts, 0, dim)
    shape = parts.shape
    return parts.reshape(*shape[:dim], shape[dim] * shape[dim + 1], *shape[dim + 2 :])


def collect(shard, axis, dim):
    parts = sent_to_all(shard, axis)
    return in_order(parts, dim)


def regret_match(positive, total_sum, option_count):
    return (positive + smooth) / (total_sum + option_count * smooth)


def leaf_piece(source, leaves, leaf_index):
    hands_total = source.shape[-1]
    share_len = -(-hands_total // leaves)
    padding = [(0, 0)] * (source.ndim - 1) + [(0, share_len * leaves - hands_total)]
    padded = jnp.pad(source, padding)
    return lax.dynamic_slice_in_dim(padded, leaf_index * share_len, share_len, source.ndim - 1)


def apply_blocks(rank_rows, live_rows, column_sets):
    hands_total = rank_rows.shape[-1]
    half_rows = hands_total // 2

    def one_block(scan_state, inputs):
        rank_row, live_row, column_set = inputs
        tile_list = []
        for offset in (0, half_rows):
            rows_rank = rank_row[offset : offset + half_rows]
            rows_live = live_row[offset : offset + half_rows]
            sign_tile = jnp.sign(rows_rank[:, None] - rank_row[None, :]).astype(jnp.bfloat16)
            matrix = sign_tile * rows_live[:, None] * live_row[None, :]
            tile_list.append(
                lax.dot_general(
                    column_set, matrix, (((1,), (1,)), ((), ())), preferred_element_type=jnp.float32
                )
            )
        return (scan_state, jnp.concatenate(tile_list, axis=1))

    unused, result = lax.scan(
        one_block, jnp.zeros((), jnp.int32), (rank_rows, live_rows, column_sets)
    )
    return result


def shards(child_row, counts, live_mask, hand_rank, bet_size, pot_size, trunk_ranges, trunk_values):
    leaves = lax.axis_size("leaf")
    leaf_index = lax.axis_index("leaf")
    hands_total = trunk_ranges.shape[-1]
    all_ranges, all_values = in_one_piece((trunk_ranges, trunk_values), SUB, 0, 1)
    ranges = jnp.take(all_ranges, child_row, axis=0)
    values = jnp.take(all_values, child_row, axis=0)
    own_range = ranges[:, 0]
    opp_range = ranges[:, 1]
    local_subs = live_mask.shape[0]
    block_count = live_mask.shape[1]
    live_real = live_mask.astype(jnp.float32)
    live_half = live_mask.astype(jnp.bfloat16).reshape(local_subs * block_count, hands_total)
    rank_rows = hand_rank.reshape(local_subs * block_count, hands_total)
    global_block = leaf_index * block_count + jnp.arange(block_count)
    block_weight = jnp.where(global_block[None, :] < counts[:, None], 1.0, 0.0) / counts[
        :, None
    ].astype(jnp.float32)
    weight = block_weight[:, :, None, None]
    factor = pot_size[:, None] * (1.0 + bet_size) / hands_total
    regret_own = jnp.zeros((local_subs, ACT, hands_total), jnp.float32)
    call_regret = jnp.zeros((local_subs, block_count, ACT, hands_total), jnp.float32)
    fold_regret = jnp.zeros((local_subs, block_count, ACT, hands_total), jnp.float32)
    follow_regret = jnp.zeros((local_subs, hands_total), jnp.float32)
    stop_regret = jnp.zeros((local_subs, hands_total), jnp.float32)
    for step_index in range(ITERS):
        own_strategy = regret_match(regret_own, jnp.sum(regret_own, axis=1, keepdims=True), ACT)
        call_prob = regret_match(call_regret, call_regret + fold_regret, 2)
        follow = regret_match(follow_regret, follow_regret + stop_regret, 2)
        reach_own = (own_range[:, None, :] * own_strategy).astype(jnp.bfloat16)
        entering = opp_range * follow
        reach_call = (entering[:, None, None, :] * call_prob).astype(jnp.bfloat16)
        reach_fold = entering[:, None, None, :] * (1.0 - call_prob)
        column_sets = jnp.concatenate(
            [reach_call, jnp.broadcast_to(reach_own[:, None], reach_call.shape)], axis=2
        )
        column_sets = column_sets.reshape(local_subs * block_count, 2 * ACT, hands_total)
        applied = apply_blocks(rank_rows, live_half, column_sets).reshape(
            local_subs, block_count, 2 * ACT, hands_total
        )
        showdown_own = applied[:, :, :ACT]
        showdown_opp = applied[:, :, ACT:]
        own_real = reach_own.astype(jnp.float32)
        fold_mass = jnp.sum(live_real[:, :, None, :] * reach_fold, axis=-1) / hands_total
        own_mass = jnp.sum(live_real[:, :, None, :] * own_real[:, None], axis=-1) / hands_total
        per_block = (
            factor[:, None, :, None] * showdown_own
            + live_real[:, :, None, :] * (pot_size[:, None, None] * fold_mass)[..., None]
        )
        partial_own = jnp.sum(weight * per_block, axis=1)
        call_value = factor[:, None, :, None] * showdown_opp
        fold_value = -live_real[:, :, None, :] * (pot_size[:, None, None] * own_mass)[..., None]
        node_value = call_prob * call_value + (1.0 - call_prob) * fold_value
        partial_follow = jnp.sum(weight * node_value, axis=(1, 2))
        value_own, follow_value = (
            taken_together(partial_own, "leaf"),
            taken_together(partial_follow, "leaf"),
        )
        gadget_value = follow * follow_value + (1.0 - follow) * values
        root_value = jnp.sum(own_strategy * value_own, axis=1)
        if step_index + 1 < ITERS:
            regret_own = jnp.maximum(regret_own + value_own - root_value[:, None, :], 0.0)
            call_regret = jnp.maximum(call_regret + call_value - node_value, 0.0)
            fold_regret = jnp.maximum(fold_regret + fold_value - node_value, 0.0)
            follow_regret = jnp.maximum(follow_regret + follow_value - gadget_value, 0.0)
            stop_regret = jnp.maximum(stop_regret + values - gadget_value, 0.0)
    results = jnp.stack([root_value, jnp.maximum(values, follow_value)], axis=1)
    total_rows = lax.axis_size(SUB) * local_subs
    hand_part = leaf_piece(results, leaves, leaf_index)
    dense_rows = (
        jnp.zeros((total_rows, 2, hand_part.shape[-1]), jnp.float32).at[child_row].set(hand_part)
    )
    summed = summed_rows(dense_rows, (("sub_0", "sub_1"), "sub_2"), 0)
    joined = collect(summed, "leaf", 2)
    answer = joined[..., :hands_total]
    return answer


def solution(mesh):
    split = Mesh(
        mesh.devices.reshape(8, 8, 2, mesh.shape["leaf"]), ("sub_0", "sub_1", "sub_2", "leaf")
    )
    in_specs = (
        P(SUB),
        P(SUB),
        P(SUB, "leaf", None),
        P(SUB, "leaf", None),
        P(SUB, None),
        P(SUB),
        P(SUB, None, None),
        P(SUB, None),
    )
    out_specs = P(SUB, None, None)
    return jax.shard_map(
        shards, mesh=split, in_specs=in_specs, out_specs=out_specs, check_vma=False
    )
```

profile of v0, /device:TPU:1, one launch (start us, length us, event | category | flops | bytes accessed | tf_op | source)
XLA Modules:
  0.0 338.1 jit_solution(11942170430266035733)
XLA Ops:
  15.4 85.4 %all-gather.3.cloned.1.call-done = f32[128,2,3978]{2,1,0:T(2,128)} async-done(((f32[1,2,3978]{2,1,0:T(2,128)}), f32[128,2,3978]{2,1,0:T(2,128)}) %all-gather.3.cloned.1.call-update) | async-done | bytes 4073488 | tf_op jit(solution)/shard_map/all_gather | solution.py:22
  100.8 6.1 %reshape.409 = f32[256,3978]{1,0:T(8,128)} reshape(f32[128,2,3978]{2,1,0:T(2,128)} %all-gather.3.cloned.1.call-done) | data formatting | bytes 8146944
  108.6 3.2 reshape.410
  114.5 22.7 %while.40 = (s32[]{:T(128)}, f32[8,16,1326]{2,1,0:T(8,128)S(1)}, bf16[8,16,1326]{2,1,0:T(8,128)(2,1)S(1)}, s32[8,1326]{1,0:T(8,128)S(1)}, bf16[8,1326]{1,0:T(8,128)(2,1)S(1)}, /*index=5*/s32[]{:T(128)}, s32[]{:T(128)}, s32[]{}) while((s32[]{:T(128)}, f32[8,16,1326]{2,1,0:T(8,128)S(1)}, bf16[8,16,1326]{2,1,0:T(8,128)(2,1)S(1)}, ...), condition=%wide.region_1.2_spmd, body=%wide.region_0.1_spmd.sunk | while | flops 65077432 | bytes 432213 | solution.py:97
  138.3 4.0 %all-to-all-start.1 = ((f32[4,2,1326]{2,1,0:T(2,128)}), f32[4,2,1326]{2,1,0:T(2,128)S(1)}, u32[]{:S(2)}, u32[]{:S(2)}) async-start(f32[4,2,1326]{2,1,0:T(2,128)} %broadcast_in_dim.99), calls=%async_computation.1 | async-start | bytes 90112 | tf_op jit(solution)/shard_map/all_to_all | solution.py:29
  147.4 3.5 %all-to-all-start = ((f32[4,2,8,1326]{3,2,1,0:T(8,128)}), f32[4,2,8,1326]{3,2,1,0:T(8,128)S(1)}, u32[]{:S(2)}, u32[]{:S(2)}) async-start(f32[4,2,8,1326]{3,2,1,0:T(8,128)} %broadcast_in_dim.98), calls=%async_computation | async-start | bytes 720896 | tf_op jit(solution)/shard_map/all_to_all | solution.py:29
  151.5 5.4 %all-to-all-done = f32[4,2,8,1326]{3,2,1,0:T(8,128)S(1)} async-done(((f32[4,2,8,1326]{3,2,1,0:T(8,128)}), f32[4,2,8,1326]{3,2,1,0:T(8,128)S(1)}, u32[]{:S(2)}, u32[]{:S(2)}) %all-to-all-start) | async-done | bytes 339488 | tf_op jit(solution)/shard_map/all_to_all | solution.py:29
  157.9 22.7 %while.41 = (s32[]{:T(128)}, f32[8,16,1326]{2,1,0:T(8,128)S(1)}, bf16[8,16,1326]{2,1,0:T(8,128)(2,1)S(1)}, s32[8,1326]{1,0:T(8,128)S(1)}, bf16[8,1326]{1,0:T(8,128)(2,1)S(1)}, /*index=5*/s32[]{:T(128)}, s32[]{:T(128)}, s32[]{}) while((s32[]{:T(128)}, f32[8,16,1326]{2,1,0:T(8,128)S(1)}, bf16[8,16,1326]{2,1,0:T(8,128)(2,1)S(1)}, ...), condition=%wide.region_11.12_spmd, body=%wide.region_10.11_spmd.sunk | while | flops 65077432 | bytes 432213 | solution.py:97
  180.8 8.4 %all_to_all.57 = f32[4,2,8,1326]{3,2,1,0:T(8,128)S(1)} all-to-all(f32[4,2,8,1326]{3,2,1,0:T(8,128)S(1)} %broadcast_in_dim.103), channel_id=1, replica_groups=mesh['sub_0'=8,'sub_1'=8,'sub_2'=2,'leaf'=4] {'leaf'}, dimensions={0} | all-to-all | bytes 678912 | tf_op jit(solution)/shard_map/all_to_all | solution.py:29
  191.3 3.5 %all-to-all-start.3 = ((f32[4,2,1326]{2,1,0:T(2,128)}), f32[4,2,1326]{2,1,0:T(2,128)S(1)}, u32[]{:S(2)}, u32[]{:S(2)}) async-start(f32[4,2,1326]{2,1,0:T(2,128)} %broadcast_in_dim.104), calls=%async_computation.3 | async-start | bytes 90112 | tf_op jit(solution)/shard_map/all_to_all | solution.py:29
  194.7 4.2 %all-to-all-done.3 = f32[4,2,1326]{2,1,0:T(2,128)S(1)} async-done(((f32[4,2,1326]{2,1,0:T(2,128)}), f32[4,2,1326]{2,1,0:T(2,128)S(1)}, u32[]{:S(2)}, u32[]{:S(2)}) %all-to-all-start.3) | async-done | bytes 42464 | tf_op jit(solution)/shard_map/all_to_all | solution.py:29
  199.6 22.7 %while.42 = (s32[]{:T(128)}, f32[8,16,1326]{2,1,0:T(8,128)S(1)}, bf16[8,16,1326]{2,1,0:T(8,128)(2,1)S(1)}, s32[8,1326]{1,0:T(8,128)S(1)}, bf16[8,1326]{1,0:T(8,128)(2,1)S(1)}, /*index=5*/s32[]{:T(128)}, s32[]{:T(128)}, s32[]{}) while((s32[]{:T(128)}, f32[8,16,1326]{2,1,0:T(8,128)S(1)}, bf16[8,16,1326]{2,1,0:T(8,128)(2,1)S(1)}, ...), condition=%wide.region_21.22_spmd, body=%wide.region_20.21_spmd.sunk | while | flops 65077432 | bytes 432213 | solution.py:97
  223.3 3.3 all-to-all-start.5
  226.6 4.3 %all-to-all-done.5 = f32[4,2,1326]{2,1,0:T(2,128)S(1)} async-done(((f32[4,2,1326]{2,1,0:T(2,128)}), f32[4,2,1326]{2,1,0:T(2,128)S(1)}, u32[]{:S(2)}, u32[]{:S(2)}) %all-to-all-start.5) | async-done | bytes 42464 | tf_op jit(solution)/shard_map/all_to_all | solution.py:29
  231.7 3.5 %all-to-all-start.4 = ((f32[4,2,8,1326]{3,2,1,0:T(8,128)}), f32[4,2,8,1326]{3,2,1,0:T(8,128)S(1)}, u32[]{:S(2)}, u32[]{:S(2)}) async-start(f32[4,2,8,1326]{3,2,1,0:T(8,128)} %broadcast_in_dim.106), calls=%async_computation.4 | async-start | bytes 720896 | tf_op jit(solution)/shard_map/all_to_all | solution.py:29
  235.3 5.9 %all-to-all-done.4 = f32[4,2,8,1326]{3,2,1,0:T(8,128)S(1)} async-done(((f32[4,2,8,1326]{3,2,1,0:T(8,128)}), f32[4,2,8,1326]{3,2,1,0:T(8,128)S(1)}, u32[]{:S(2)}, u32[]{:S(2)}) %all-to-all-start.4) | async-done | bytes 339488 | tf_op jit(solution)/shard_map/all_to_all | solution.py:29
  242.9 22.7 %while.43 = (s32[]{:T(128)}, f32[8,16,1326]{2,1,0:T(8,128)S(1)}, bf16[8,16,1326]{2,1,0:T(8,128)(2,1)S(1)}, s32[8,1326]{1,0:T(8,128)S(1)}, bf16[8,1326]{1,0:T(8,128)(2,1)S(1)}, /*index=5*/s32[]{:T(128)}, s32[]{:T(128)}, s32[]{}) while((s32[]{:T(128)}, f32[8,16,1326]{2,1,0:T(8,128)S(1)}, bf16[8,16,1326]{2,1,0:T(8,128)(2,1)S(1)}, ...), condition=%wide.region_31.32_spmd, body=%wide.region_30.31_spmd.sunk | while | flops 65077432 | bytes 432213 | solution.py:97
  266.6 3.3 all-to-all-start.7
  269.9 4.3 %all-to-all-done.7 = f32[4,2,1326]{2,1,0:T(2,128)S(1)} async-done(((f32[4,2,1326]{2,1,0:T(2,128)}), f32[4,2,1326]{2,1,0:T(2,128)S(1)}, u32[]{:S(2)}, u32[]{:S(2)}) %all-to-all-start.7) | async-done | bytes 42464 | tf_op jit(solution)/shard_map/all_to_all | solution.py:29
  274.9 3.5 %all-to-all-start.6 = ((f32[4,2,8,1326]{3,2,1,0:T(8,128)}), f32[4,2,8,1326]{3,2,1,0:T(8,128)S(1)}, u32[]{:S(2)}, u32[]{:S(2)}) async-start(f32[4,2,8,1326]{3,2,1,0:T(8,128)} %broadcast_in_dim.109), calls=%async_computation.6 | async-start | bytes 720896 | tf_op jit(solution)/shard_map/all_to_all | solution.py:29
  278.5 5.9 %all-to-all-done.6 = f32[4,2,8,1326]{3,2,1,0:T(8,128)S(1)} async-done(((f32[4,2,8,1326]{3,2,1,0:T(8,128)}), f32[4,2,8,1326]{3,2,1,0:T(8,128)S(1)}, u32[]{:S(2)}, u32[]{:S(2)}) %all-to-all-start.6) | async-done | bytes 339488 | tf_op jit(solution)/shard_map/all_to_all | solution.py:29
  285.7 13.8 %all_to_all.55 = f32[2,64,2,2,332]{4,3,2,1,0:T(2,128)S(1)} all-to-all(f32[2,64,2,2,332]{4,3,2,1,0:T(2,128)S(1)} %bitcast.108), channel_id=1, replica_groups=mesh['sub_0'=8,'sub_1'=8,'sub_2'=2,'leaf'=4] {'sub_2'}, dimensions={0} | all-to-all | bytes 1359872 | tf_op jit(solution)/shard_map/all_to_all | solution.py:45
  300.2 23.6 %all_to_all.58 = f32[64,2,2,332]{3,2,1,0:T(2,128)S(1)} all-to-all(f32[64,2,2,332]{3,2,1,0:T(2,128)S(1)} %reduce_sum.335), channel_id=1, replica_groups=mesh['sub_0'=8,'sub_1'=8,'sub_2'=2,'leaf'=4] {'sub_0','sub_1'}, dimensions={0} | all-to-all | bytes 679936 | tf_op jit(solution)/shard_map/all_to_all | solution.py:52
  324.0 6.6 %all_to_all.56 = f32[4,2,2,332]{3,2,1,0:T(2,128)S(1)} all-to-all(f32[4,2,2,332]{3,2,1,0:T(2,128)S(1)} %broadcast_in_dim.121), channel_id=1, replica_groups=mesh['sub_0'=8,'sub_1'=8,'sub_2'=2,'leaf'=4] {'leaf'}, dimensions={0} | all-to-all | bytes 42496 | tf_op jit(solution)/shard_map/all_to_all | solution.py:29
  (321 shorter events, 122.4 us)
Async XLA Ops:
  6.5 94.3 %all-gather.3.cloned.1.call-start = ((), (), s32[]{:S(2)}) async-start(), calls=%async_computation.11 | async-start | bytes 4227072 | tf_op jit(solution)/shard_map/all_gather | solution.py:22
  106.9 1.8 slice-start
  138.3 8.3 %all-to-all-start.1 = ((f32[4,2,1326]{2,1,0:T(2,128)}), f32[4,2,1326]{2,1,0:T(2,128)S(1)}, u32[]{:S(2)}, u32[]{:S(2)}) async-start(f32[4,2,1326]{2,1,0:T(2,128)} %broadcast_in_dim.99), calls=%async_computation.1 | async-start | bytes 90112 | tf_op jit(solution)/shard_map/all_to_all | solution.py:29
  147.4 9.5 %all-to-all-start = ((f32[4,2,8,1326]{3,2,1,0:T(8,128)}), f32[4,2,8,1326]{3,2,1,0:T(8,128)S(1)}, u32[]{:S(2)}, u32[]{:S(2)}) async-start(f32[4,2,8,1326]{3,2,1,0:T(8,128)} %broadcast_in_dim.98), calls=%async_computation | async-start | bytes 720896 | tf_op jit(solution)/shard_map/all_to_all | solution.py:29
  191.3 7.6 %all-to-all-start.3 = ((f32[4,2,1326]{2,1,0:T(2,128)}), f32[4,2,1326]{2,1,0:T(2,128)S(1)}, u32[]{:S(2)}, u32[]{:S(2)}) async-start(f32[4,2,1326]{2,1,0:T(2,128)} %broadcast_in_dim.104), calls=%async_computation.3 | async-start | bytes 90112 | tf_op jit(solution)/shard_map/all_to_all | solution.py:29
  223.3 7.6 %all-to-all-start.5 = ((f32[4,2,1326]{2,1,0:T(2,128)}), f32[4,2,1326]{2,1,0:T(2,128)S(1)}, u32[]{:S(2)}, u32[]{:S(2)}) async-start(f32[4,2,1326]{2,1,0:T(2,128)} %broadcast_in_dim.107), calls=%async_computation.5 | async-start | bytes 90112 | tf_op jit(solution)/shard_map/all_to_all | solution.py:29
  231.7 9.5 %all-to-all-start.4 = ((f32[4,2,8,1326]{3,2,1,0:T(8,128)}), f32[4,2,8,1326]{3,2,1,0:T(8,128)S(1)}, u32[]{:S(2)}, u32[]{:S(2)}) async-start(f32[4,2,8,1326]{3,2,1,0:T(8,128)} %broadcast_in_dim.106), calls=%async_computation.4 | async-start | bytes 720896 | tf_op jit(solution)/shard_map/all_to_all | solution.py:29
  266.6 7.6 %all-to-all-start.7 = ((f32[4,2,1326]{2,1,0:T(2,128)}), f32[4,2,1326]{2,1,0:T(2,128)S(1)}, u32[]{:S(2)}, u32[]{:S(2)}) async-start(f32[4,2,1326]{2,1,0:T(2,128)} %broadcast_in_dim.112), calls=%async_computation.7 | async-start | bytes 90112 | tf_op jit(solution)/shard_map/all_to_all | solution.py:29
  274.9 9.5 %all-to-all-start.6 = ((f32[4,2,8,1326]{3,2,1,0:T(8,128)}), f32[4,2,8,1326]{3,2,1,0:T(8,128)S(1)}, u32[]{:S(2)}, u32[]{:S(2)}) async-start(f32[4,2,8,1326]{3,2,1,0:T(8,128)} %broadcast_in_dim.109), calls=%async_computation.6 | async-start | bytes 720896 | tf_op jit(solution)/shard_map/all_to_all | solution.py:29
Sparse Core Ops, SparseCore 0:
  10.5 90.2 all-gather.2
where the time goes:
time: 341 us; the launch traced here: 338 us
  waiting for transfers between devices  117 us (34%)
  matrix products  77.8 us (23%)
  blocking collectives  52.4 us (15%)
  local copies, waits for them, and re-layouts  33.1 us (10%)
  starting transfers between devices  24.3 us (7%)
  other arithmetic  18.8 us (6%)
  between operations  13.8 us (4%)
    all_gather x1, waiting for transfers between devices, in_one_piece(): whole = lax.all_gather(both, axis, axis=dim, tiled=True)  85.4 us
    dot_general x64, matrix products, one_block(): lax.dot_general(column_set, matrix, (((1,), (1,)), ((), ())), preferred_e...  77.8 us
    all_to_all x7, waiting for transfers between devices, sent_to_all(): return lax.all_to_all(copies, axis, split_axis=0, concat_axis=0, tiled=True)  32 us
    all_to_all x7, starting transfers between devices, sent_to_all(): return lax.all_to_all(copies, axis, split_axis=0, concat_axis=0, tiled=True)  24.3 us
    all_to_all x1, blocking collectives, summed_rows(): return jnp.sum(lax.all_to_all(own, far, 0, 0, tiled=True), axis=0)  23.6 us
    all_to_all x2, blocking collectives, sent_to_all(): return lax.all_to_all(copies, axis, split_axis=0, concat_axis=0, tiled=True)  15 us
    all_to_all x1, blocking collectives, summed_on_arrival(): lax.all_to_all(parts, axis, split_axis=0, concat_axis=0, tiled=True)  13.8 us
  transfers between devices with their start and end apart: 8, of which 8 were waited for; matrix products, arithmetic and copies ran while one was open for 3% of the time, Pallas kernels for 0%

commit v1 on v0

v1 whole, which is shorter than its diff:
```python
import jax
import jax.numpy as jnp
from jax import lax
from jax.experimental import pallas as pl
from jax.experimental.pallas import tpu as pltpu
from jax.sharding import Mesh
from jax.sharding import PartitionSpec as P

ACT = 8
ITERS = 4
BLOCKS = 16
SUB = ("z", "y", "c")
NZ, NY, NC, NX = 8, 8, 2, 4
LANES = 128
smooth = 0.1
F32 = jnp.float32
BF16 = jnp.bfloat16
F8 = jnp.float8_e4m3fn
SMEM = pl.BlockSpec(memory_space=pltpu.SMEM)
VMEM = pl.BlockSpec(memory_space=pltpu.VMEM)


def round_up(value, unit):
    return -(-value // unit) * unit


def row_parts(row):
    slot = lax.rem(row, 2)
    core = lax.rem(lax.div(row, 2), NC)
    y = lax.rem(lax.div(row, 2 * NC), NY)
    z = lax.div(row, 2 * NC * NY)
    return z, y, core, slot


def pack_rows(ids_ref, ranges_ref, values_ref, out_ref, rows_ref):
    hands = values_ref.shape[-1]
    full = hands // LANES
    rest = hands - full * LANES
    x = ids_ref[3]
    rows_ref[...] = jnp.zeros(rows_ref.shape, F32)
    for s in range(2):
        sources = (ranges_ref[s, 0:1, :], ranges_ref[s, 1:2, :], values_ref[s : s + 1, :])
        for v, line in enumerate(sources):
            for r in range(full):
                at = v * full + r
                rows_ref[s, at : at + 1, :] = line[:, r * LANES : (r + 1) * LANES]
            tail_row = 3 * full + v // 2
            tail_lane = (v % 2) * (LANES // 2)
            rows_ref[s, tail_row : tail_row + 1, tail_lane : tail_lane + rest] = line[:, full * LANES :]
    for s in range(2):
        piece = rows_ref[s, pl.ds(pl.multiple_of(8 * x, 8), 8), :]
        for d in range(out_ref.shape[0]):
            out_ref[d, s] = piece


def select_rows(wants_ref, arrived_ref, out_ref):
    for y in range(NY):
        for k in range(2):
            z, _, core, slot = row_parts(wants_ref[y, k])
            piece = arrived_ref[z * NC + core, slot]
            for x in (2 * k, 2 * k + 1):
                out_ref[y, x] = piece


def solve_kernel(
    ids_ref, child_ref, counts_ref, bet_ref, pot_ref, blocks_ref, rows_ref, out_ref,
    rank_ref, live_ref, sign_ref, column_ref, vec_ref, lhs_ref, prob_ref, call_ref, fold_ref, pack_ref,
):
    hands = blocks_ref.shape[-1]
    full = hands // LANES
    rest = hands - full * LANES
    width = rank_ref.shape[-1]
    deep = lhs_ref.shape[-1]
    core = ids_ref[2]
    x = ids_ref[3]
    k = lax.div(x, 2)
    active = lax.rem(x, 2) == core
    count = jnp.where(active, counts_ref[k], 0)
    pot = pot_ref[k]

    rank_ref[...] = jnp.zeros(rank_ref.shape, F32)
    live_ref[...] = jnp.zeros(live_ref.shape, F32)
    for source in range(NX):
        rank_ref[4 * source : 4 * source + 4, 0:hands] = blocks_ref[source, 0].astype(F32)
        live_ref[4 * source : 4 * source + 4, 0:hands] = blocks_ref[source, 1].astype(F32)

    for t in range(width // LANES):
        column_ref[t * LANES : (t + 1) * LANES, :] = rank_ref[:, t * LANES : (t + 1) * LANES].T
    tall = round_up(hands, 32)
    for b in range(BLOCKS):

        @pl.when(b < count)
        def _():
            line = rank_ref[b : b + 1, :]

            def chunk(q, carry):
                at = pl.multiple_of(q * 32, 32)
                column = column_ref[pl.ds(at, 32), b : b + 1]
                signs = jnp.clip(line - column, -1.0, 1.0)
                sign_ref[b, pl.ds(at, 32), 0:width] = signs.astype(F8)
                return carry

            lax.fori_loop(0, tall // 32, chunk, 0, unroll=2)
            sign_ref[b, tall:deep, :] = jnp.zeros((deep - tall, deep), F8)

    _, y, _, _ = row_parts(child_ref[k])
    vec_ref[...] = jnp.zeros(vec_ref.shape, F32)
    for v in range(3):
        for r in range(full):
            at = v * full + r
            vec_ref[v : v + 1, r * LANES : (r + 1) * LANES] = rows_ref[y, at // 8, at % 8 : at % 8 + 1, :]
        at = 3 * full + v // 2
        tail = rows_ref[y, at // 8, at % 8 : at % 8 + 1, :]
        if v % 2:
            tail = pltpu.roll(tail, LANES // 2, 1)
        vec_ref[v : v + 1, full * LANES : hands] = tail[:, 0:rest]
    own_range = vec_ref[0:1, :]
    opp_range = vec_ref[1:2, :]
    values = vec_ref[2:3, :]

    lane_rows = lax.broadcasted_iota(jnp.int32, (ACT, 1), 0)
    bets = jnp.zeros((ACT, 1), F32)
    for a in range(ACT):
        bets = jnp.where(lane_rows == a, bet_ref[k, a], bets)
    factor = pot * (1.0 + bets) / hands
    weight = 1.0 / jnp.broadcast_to(count.astype(F32), (1, 1))
    lhs_ref[:, width:deep] = jnp.zeros((2 * ACT, deep - width), BF16)

    regret_own = jnp.zeros((ACT, width), F32)
    follow_regret = jnp.zeros((1, width), F32)
    stop_regret = jnp.zeros((1, width), F32)
    for step in range(ITERS):
        first = step == 0
        last = step + 1 == ITERS
        strategy = (regret_own + smooth) / (jnp.sum(regret_own, axis=0, keepdims=True) + ACT * smooth)
        follow = (follow_regret + smooth) / (follow_regret + stop_regret + 2 * smooth)
        entering = opp_range * follow
        reach_own = (own_range * strategy).astype(BF16).astype(F32)

        def block(b, carry):
            value_sum, node_sum = carry
            live = live_ref[pl.ds(b, 1), :]
            prob = jnp.full((ACT, width), 0.5, F32) if first else prob_ref[b]
            live_own = reach_own * live
            lhs_ref[0:ACT, 0:width] = (entering * prob).astype(BF16) * live.astype(BF16)
            lhs_ref[ACT : 2 * ACT, 0:width] = live_own.astype(BF16)
            fold_mass = jnp.sum(live * (entering * (1.0 - prob)), axis=1, keepdims=True) / hands
            own_mass = jnp.sum(live_own, axis=1, keepdims=True) / hands

            def multiply(*sums):
                for n in range(deep // 256):
                    for j in range(deep // 256):
                        tile = sign_ref[b, 256 * j : 256 * (j + 1), 256 * n : 256 * (n + 1)]
                        pltpu.matmul_push_rhs(tile, staging_register=j % 2, mxu_index=n % 2)
                        pltpu.matmul_acc_lhs(sums[n], lhs_ref[:, 256 * j : 256 * (j + 1)], load_staged_rhs=j % 2)
                return jnp.concatenate([pltpu.matmul_pop(s) for s in sums], axis=1)[:, :width]

            applied = pl.run_scoped(
                multiply, *[pltpu.ACC(n % 2)((2 * ACT, 256), F32) for n in range(deep // 256)]
            )
            showdown_own = applied[0:ACT] * live
            showdown_opp = applied[ACT : 2 * ACT] * live
            value_sum = value_sum + weight * (factor * showdown_own + live * (pot * fold_mass))
            call_value = factor * showdown_opp
            fold_value = -live * (pot * own_mass)
            node_value = prob * call_value + (1.0 - prob) * fold_value
            node_sum = node_sum + weight * node_value
            if not last:
                call = call_value - node_value
                fold = fold_value - node_value
                if not first:
                    call = call_ref[b] + call
                    fold = fold_ref[b] + fold
                call = jnp.maximum(call, 0.0)
                fold = jnp.maximum(fold, 0.0)
                call_ref[b] = call
                fold_ref[b] = fold
                prob_ref[b] = (call + smooth) / (call + fold + 2 * smooth)
            return value_sum, node_sum

        zeros = jnp.zeros((ACT, width), F32)
        value_own, node_sum = lax.fori_loop(0, count, block, (zeros, zeros))
        follow_value = jnp.sum(node_sum, axis=0, keepdims=True)
        gadget_value = follow * follow_value + (1.0 - follow) * values
        root_value = jnp.sum(strategy * value_own, axis=0, keepdims=True)
        if not last:
            regret_own = jnp.maximum(regret_own + value_own - root_value, 0.0)
            follow_regret = jnp.maximum(follow_regret + follow_value - gadget_value, 0.0)
            stop_regret = jnp.maximum(stop_regret + values - gadget_value, 0.0)

    pack_ref[...] = jnp.zeros(pack_ref.shape, F32)
    for v, line in enumerate((root_value, jnp.maximum(values, follow_value))):
        for r in range(full):
            at = v * full + r
            pack_ref[at // 6, at % 6 : at % 6 + 1, :] = line[:, r * LANES : (r + 1) * LANES]
        at = 2 * full
        lane = v * (LANES // 2)
        pack_ref[at // 6, at % 6 : at % 6 + 1, lane : lane + rest] = line[:, full * LANES : hands]
    for y in range(NY):
        out_ref[y] = pack_ref[...]


def route_results(ids_ref, wants_ref, arrived_ref, out_ref):
    here = ids_ref[1]
    core_here = ids_ref[2]
    out_ref[...] = jnp.zeros(out_ref.shape, F32)
    for y in range(NY):
        for k in range(2):
            z, row_y, core, slot = row_parts(wants_ref[y, k])

            @pl.when(row_y == here)
            def _():
                piece = arrived_ref[y, 2 * k + core_here]
                for x in range(NX):
                    out_ref[(z * NC + core) * NX + x, slot] = piece


def unpack_results(arrived_ref, out_ref):
    hands = out_ref.shape[-1]
    full = hands // LANES
    rest = hands - full * LANES
    for s in range(2):
        lines = []
        for x in range(NX):
            total = arrived_ref[x, s]
            for source in range(1, NZ * NC):
                total = total + arrived_ref[source * NX + x, s]
            lines.append(total)
        for v in range(2):
            for r in range(full):
                at = v * full + r
                out_ref[s, v : v + 1, r * LANES : (r + 1) * LANES] = lines[at // 6][at % 6 : at % 6 + 1, :]
            at = 2 * full
            tail = lines[at // 6][at % 6 : at % 6 + 1, :]
            if v:
                tail = pltpu.roll(tail, LANES // 2, 1)
            out_ref[s, v : v + 1, full * LANES : hands] = tail[:, 0:rest]


def exchange(parts, axes):
    return lax.all_to_all(parts, axes, split_axis=0, concat_axis=0, tiled=True)


def shards(child_row, counts, live_mask, hand_rank, bet_size, pot_size, trunk_ranges, trunk_values):
    hands = trunk_ranges.shape[-1]
    width = round_up(hands, LANES)
    deep = round_up(hands, 256)
    ids = jnp.stack([lax.axis_index(a) for a in ("z", "y", "c", "leaf")])

    packed = pl.pallas_call(
        pack_rows,
        out_shape=jax.ShapeDtypeStruct((NZ * NC, 2, 8, LANES), F32),
        in_specs=[SMEM, VMEM, VMEM],
        out_specs=VMEM,
        scratch_shapes=[pltpu.VMEM((2, 32, LANES), F32)],
        name="pack_rows",
    )(ids, trunk_ranges, trunk_values)
    gathered = exchange(packed, ("z", "c"))
    wants = exchange(jnp.broadcast_to(child_row, (NY, 2)), "y")
    both = jnp.stack([hand_rank, live_mask], axis=1)
    blocks = exchange(jnp.repeat(both, 2, axis=0), "leaf")
    selected = pl.pallas_call(
        select_rows,
        out_shape=jax.ShapeDtypeStruct((NY, NX, 8, LANES), F32),
        in_specs=[SMEM, VMEM],
        out_specs=VMEM,
        name="select_rows",
    )(wants, gathered)
    rows = exchange(selected.reshape(NY * NX, 8, LANES), ("y", "leaf")).reshape(NY, NX, 8, LANES)
    results = pl.pallas_call(
        solve_kernel,
        out_shape=jax.ShapeDtypeStruct((NY, NX, 8, LANES), F32),
        in_specs=[SMEM, SMEM, SMEM, SMEM, SMEM, VMEM, VMEM],
        out_specs=VMEM,
        scratch_shapes=[
            pltpu.VMEM((BLOCKS, width), F32),
            pltpu.VMEM((BLOCKS, width), F32),
            pltpu.VMEM((BLOCKS, deep, deep), F8),
            pltpu.VMEM((width, BLOCKS), F32),
            pltpu.VMEM((8, width), F32),
            pltpu.VMEM((2 * ACT, deep), BF16),
            pltpu.VMEM((BLOCKS, ACT, width), F32),
            pltpu.VMEM((BLOCKS, ACT, width), F32),
            pltpu.VMEM((BLOCKS, ACT, width), F32),
            pltpu.VMEM((NX, 8, LANES), F32),
        ],
        compiler_params=pltpu.CompilerParams(vmem_limit_bytes=56 * 1024 * 1024),
        name="solve",
    )(ids, child_row, counts, bet_size, pot_size, blocks, rows)
    back = exchange(results.reshape(NY * NX, 8, LANES), ("y", "leaf")).reshape(NY, NX, 8, LANES)
    routed = pl.pallas_call(
        route_results,
        out_shape=jax.ShapeDtypeStruct((NZ * NC * NX, 2, 8, LANES), F32),
        in_specs=[SMEM, SMEM, VMEM],
        out_specs=VMEM,
        name="route_results",
    )(ids, wants, back)
    home = exchange(routed, ("z", "c", "leaf"))
    return pl.pallas_call(
        unpack_results,
        out_shape=jax.ShapeDtypeStruct(trunk_ranges.shape, F32),
        in_specs=[VMEM],
        out_specs=VMEM,
        name="unpack_results",
    )(home)


def solution(mesh):
    split = Mesh(mesh.devices.reshape(NZ, NY, NC, NX), ("z", "y", "c", "leaf"))
    in_specs = (
        P(SUB),
        P(SUB),
        P(SUB, "leaf", None),
        P(SUB, "leaf", None),
        P(SUB, None),
        P(SUB),
        P(SUB, None, None),
        P(SUB, None),
    )
    return jax.shard_map(
        shards, mesh=split, in_specs=in_specs, out_specs=P(SUB, None, None), check_vma=False
    )
```

time: 341 us -> 169 us (0.50)
  waiting for transfers between devices: 117 us -> 17 us
  matrix products: 77.8 us -> 0 us
  blocking collectives: 52.4 us -> 114 us
  local copies, waits for them, and re-layouts: 33.1 us -> 2.6 us
  other arithmetic: 18.8 us -> 0.66 us
  between operations: 13.8 us -> 0.04 us
  Pallas kernels: 0 us -> 9.31 us
    all_gather x1 -> x0, waiting for transfers between devices: 85.4 us -> none  [in_one_piece(): whole = lax.all_gather(both, axis, axis=dim, tiled=True)]
    dot_general x64 -> x0, matrix products: 77.8 us -> none  [one_block(): lax.dot_general(column_set, matrix, (((1,), (1,)), ((), ())), preferred_e...]
    all_to_all x4 -> x3, blocking collectives: 52.4 us -> 114 us  [exchange(): return lax.all_to_all(parts, axes, split_axis=0, concat_axis=0, tiled=True)]
    all_to_all x7 -> x3, waiting for transfers between devices: 32 us -> 17 us  [exchange(): return lax.all_to_all(parts, axes, split_axis=0, concat_axis=0, tiled=True)]
    pallas_call x0 -> x5, Pallas kernels: none -> 9.31 us  [the longest x1 2.43 us: shards(): pl.pallas_call(solve_kernel, out_shape=jax.ShapeDtypeStruct((NY, NX, 8, L...]
    slice x65 -> x0, local copies, waits for them, and re-layouts: 6.63 us -> none  [the longest x32 3.44 us: one_block(): rows_live = live_row[offset:offset + half_rows]]
    reshape x5 -> x0, local copies, waits for them, and re-layouts: 5.6 us -> none  [the longest x1 3.23 us: in_one_piece(): b.reshape(*whole.shape[:along], *a.shape[along:])]
    unnamed x2 -> x10, local copies, waits for them, and re-layouts: 6.07 us -> 0.61 us
  transfers between devices with their start and end apart: 8 -> 3, of which waited for: 8 -> 3; matrix products, arithmetic and copies ran while one was open for 3% -> 0% of each run, Pallas kernels for 0% -> 2%
where the time goes in v1:
time: 169 us; the launch traced here: 168 us
  blocking collectives  114 us (67%)
  starting transfers between devices  24.1 us (14%)
  waiting for transfers between devices  17 us (10%)
  Pallas kernels  9.31 us (6%)
  local copies, waits for them, and re-layouts  2.6 us (2%)
    all_to_all x3, blocking collectives, exchange(): return lax.all_to_all(parts, axes, split_axis=0, concat_axis=0, tiled=True)  114 us
    all_to_all x3, starting transfers between devices, exchange(): return lax.all_to_all(parts, axes, split_axis=0, concat_axis=0, tiled=True)  24.1 us
    all_to_all x3, waiting for transfers between devices, exchange(): return lax.all_to_all(parts, axes, split_axis=0, concat_axis=0, tiled=True)  17 us
  transfers between devices with their start and end apart: 3, of which 3 were waited for; matrix products, arithmetic and copies ran while one was open for 0% of the time, Pallas kernels for 2%

profile of v1, /device:TPU:1, one launch (start us, length us, event | category | flops | bytes accessed | tf_op | source)
XLA Modules:
  0.0 168.2 jit_solution(8083439904972226890)
XLA Ops:
  0.0 1.2 broadcast_in_dim.6
  1.2 7.6 %all-to-all-start = ((s32[8,1,2]{2,1,0:T(1,128)}), s32[8,1,2]{2,1,0:T(1,128)S(1)}, u32[]{:S(2)}, u32[]{:S(2)}) async-start(s32[8,1,2]{2,1,0:T(1,128)} %broadcast_in_dim.6), calls=%async_computation | async-start | bytes 8192 | tf_op jit(solution)/shard_map/all_to_all | solution.py:241
  8.9 0.7 pad_add_fusion.1.ids_ref
  9.5 1.5 pack_rows.1
  11.0 0.0 copy-start.2
  11.0 0.0 copy-start.3
  11.0 4.4 %all-to-all-done = s32[8,1,2]{2,1,0:T(1,128)S(1)} async-done(((s32[8,1,2]{2,1,0:T(1,128)}), s32[8,1,2]{2,1,0:T(1,128)S(1)}, u32[]{:S(2)}, u32[]{:S(2)}) %all-to-all-start) | async-done | bytes 96 | tf_op jit(solution)/shard_map/all_to_all | solution.py:241
  15.4 0.6 copy-done.4
  16.0 12.4 %all-to-all-start.2 = ((f32[16,2,8,128]{3,2,1,0:T(8,128)}), f32[16,2,8,128]{3,2,1,0:T(8,128)S(1)}, u32[]{:S(2)}, u32[]{:S(2)}) async-start(f32[16,2,8,128]{3,2,1,0:T(8,128)} %pack_rows.1), calls=%async_computation.2 | async-start | bytes 262144 | tf_op jit(solution)/shard_map/all_to_all | solution.py:241
  28.4 0.0 copy-done.2
  28.4 0.0 copy-done.3
  28.4 8.8 %all-to-all-done.2.arrived_ref = f32[16,2,8,128]{3,2,1,0:T(8,128)S(1)} async-done(((f32[16,2,8,128]{3,2,1,0:T(8,128)}), f32[16,2,8,128]{3,2,1,0:T(8,128)S(1)}, u32[]{:S(2)}, u32[]{:S(2)}) %all-to-all-start.2) | async-done | bytes 131104 | tf_op jit(solution)/shard_map/all_to_all | solution.py:241
  37.3 0.7 broadcast_in_dim.7
  38.0 0.0 copy-done.1
  38.0 4.0 %all-to-all-start.1 = ((s32[4,2,4,1326]{3,2,1,0:T(4,128)}), s32[4,2,4,1326]{3,2,1,0:T(4,128)S(1)}, u32[]{:S(2)}, u32[]{:S(2)}) async-start(s32[4,2,4,1326]{3,2,1,0:T(4,128)} %bitcast.7), calls=%async_computation.1 | async-start | bytes 360448 | tf_op jit(solution)/shard_map/all_to_all | solution.py:241
  42.0 1.7 select_rows.1
  43.7 3.8 %all-to-all-done.1.blocks_ref = s32[4,2,4,1326]{3,2,1,0:T(4,128)S(1)} async-done(((s32[4,2,4,1326]{3,2,1,0:T(4,128)}), s32[4,2,4,1326]{3,2,1,0:T(4,128)S(1)}, u32[]{:S(2)}, u32[]{:S(2)}) %all-to-all-start.1) | async-done | bytes 169760 | tf_op jit(solution)/shard_map/all_to_all | solution.py:241
  47.5 13.9 %all_to_all.33 = f32[32,8,128]{2,1,0:T(8,128)} all-to-all(f32[32,8,128]{2,1,0:T(8,128)} %bitcast.14), channel_id=1, replica_groups=mesh['z'=8,'y'=8,'c'=2,'leaf'=4] {'y','leaf'}, dimensions={0} | all-to-all | bytes 262144 | tf_op jit(solution)/shard_map/all_to_all | solution.py:241
  61.4 0.0 copy-done
  61.4 2.4 %solve.1 = f32[8,4,8,128]{3,2,1,0:T(8,128)} custom-call(s32[4]{0:T(128)} %pad_add_fusion.1.ids_ref, s32[2]{0:T(128)} %child_ref.1, s32[2]{0:T(128)} %counts_ref.1, f32[2,8]{1,0:T(2,128)} %bet_ref.1, f32[2]{0:T(128)} %pot_ref.1, s32[4,2,4,1326]{3,2,1,0:T(4,128)} %copy-done, f32[8,4,8,128]{3,2,1,0:T(8,128)} %bitcast.12), custom_call_target="tpu_custom_call" | custom-call | tf_op jit(solution)/shard_map/solve/pallas_call | solution.py:270
  63.9 72.4 %all_to_all.34 = f32[32,8,128]{2,1,0:T(8,128)} all-to-all(f32[32,8,128]{2,1,0:T(8,128)} %bitcast.13), channel_id=1, replica_groups=mesh['z'=8,'y'=8,'c'=2,'leaf'=4] {'y','leaf'}, dimensions={0} | all-to-all | bytes 262144 | tf_op jit(solution)/shard_map/all_to_all | solution.py:241
  136.3 2.0 %route_results.1 = f32[64,2,8,128]{3,2,1,0:T(8,128)} custom-call(s32[4]{0:T(128)} %pad_add_fusion.1.ids_ref, s32[8,2]{1,0:T(8,128)} %bitcast.19, f32[8,4,8,128]{3,2,1,0:T(8,128)} %bitcast.15), custom_call_target="tpu_custom_call" | custom-call | tf_op jit(solution)/shard_map/route_results/pallas_call | solution.py:291
  138.3 28.1 %all_to_all.35.arrived_ref = f32[64,2,8,128]{3,2,1,0:T(8,128)} all-to-all(f32[64,2,8,128]{3,2,1,0:T(8,128)} %route_results.1), channel_id=1, replica_groups=mesh['z'=8,'y'=8,'c'=2,'leaf'=4] {'z','c','leaf'}, dimensions={0} | all-to-all | bytes 1048576 | tf_op jit(solution)/shard_map/all_to_all | solution.py:241
  166.4 1.8 %unpack_results.1 = f32[2,2,1326]{2,1,0:T(2,128)} custom-call(f32[64,2,8,128]{3,2,1,0:T(8,128)} %all_to_all.35.arrived_ref), custom_call_target="tpu_custom_call" | custom-call | tf_op jit(solution)/shard_map/unpack_results/pallas_call | solution.py:299
  (5 shorter events, 0.0 us)
Async XLA Ops:
  1.2 14.1 %all-to-all-start = ((s32[8,1,2]{2,1,0:T(1,128)}), s32[8,1,2]{2,1,0:T(1,128)S(1)}, u32[]{:S(2)}, u32[]{:S(2)}) async-start(s32[8,1,2]{2,1,0:T(1,128)} %broadcast_in_dim.6), calls=%async_computation | async-start | bytes 8192 | tf_op jit(solution)/shard_map/all_to_all | solution.py:241
  11.0 17.4 %copy-start.2 = (s32[2,4,1326]{2,1,0:T(4,128)S(1)}, s32[2,4,1326]{2,1,0:T(4,128)}, u32[]{:S(2)}) copy-start(s32[2,4,1326]{2,1,0:T(4,128)} %param.10) | copy-start | bytes 127300
  11.0 17.4 %copy-start.3 = (s32[2,4,1326]{2,1,0:T(4,128)S(1)}, s32[2,4,1326]{2,1,0:T(4,128)}, u32[]{:S(2)}) copy-start(s32[2,4,1326]{2,1,0:T(4,128)} %param.11) | copy-start | bytes 127300
  15.4 0.6 copy-start.4
  16.0 21.3 %all-to-all-start.2 = ((f32[16,2,8,128]{3,2,1,0:T(8,128)}), f32[16,2,8,128]{3,2,1,0:T(8,128)S(1)}, u32[]{:S(2)}, u32[]{:S(2)}) async-start(f32[16,2,8,128]{3,2,1,0:T(8,128)} %pack_rows.1), calls=%async_computation.2 | async-start | bytes 262144 | tf_op jit(solution)/shard_map/all_to_all | solution.py:241
  37.3 0.7 copy-start.1
  38.0 9.5 %all-to-all-start.1 = ((s32[4,2,4,1326]{3,2,1,0:T(4,128)}), s32[4,2,4,1326]{3,2,1,0:T(4,128)S(1)}, u32[]{:S(2)}, u32[]{:S(2)}) async-start(s32[4,2,4,1326]{3,2,1,0:T(4,128)} %bitcast.7), calls=%async_computation.1 | async-start | bytes 360448 | tf_op jit(solution)/shard_map/all_to_all | solution.py:241
  47.5 13.9 %copy-start = (s32[4,2,4,1326]{3,2,1,0:T(4,128)}, s32[4,2,4,1326]{3,2,1,0:T(4,128)S(1)}, u32[]{:S(2)}) copy-start(s32[4,2,4,1326]{3,2,1,0:T(4,128)S(1)} %all-to-all-done.1.blocks_ref) | copy-start | bytes 509188
